TPU v7x, 32 devices: a whole 2x2x4 slice. The times are simulated.
32 devices in a mesh: tp: 8 (over z, y), dp: 4 (over x, core).
Axes of the slice: x: 2, y: 2, z: 4, core: 2. Of those that a mesh axis runs over, the one named last changes fastest.
Arguments:
- tokens: bfloat16 [768, 4096], P(('dp', 'tp')), may hold values from -6 to 6
- hidden_grad: bfloat16 [768, 14336], P('dp', 'tp'), may hold values from -0.59765625 to 0.59765625
- gate_value: bfloat16 [768, 14336], P('dp', 'tp'), may hold values from -6 to 6
- up_value: bfloat16 [768, 14336], P('dp', 'tp'), may hold values from -6 to 6
- gate_weight: bfloat16 [4096, 14336], P('dp', 'tp'), may hold values from -0.09375 to 0.09375
- up_weight: bfloat16 [4096, 14336], P('dp', 'tp'), may hold values from -0.09375 to 0.09375
Outputs:
- input_grad: bfloat16 [768, 4096], P(('dp', 'tp'))
- gate_grad: bfloat16 [4096, 14336], P('dp', 'tp')
- up_grad: bfloat16 [4096, 14336], P('dp', 'tp')
All inputs are finite; a program needn't handle non-finite values.
Results may differ from a plain program's by a relative error of at most 0.018.
Values may be sent and summed in bfloat16 or wider, within the bound.
A program may use at most 128 MiB of HBM per device.

v0:
```python
import jax
import jax.numpy as jnp
from jax import lax
from jax.sharding import PartitionSpec as P


def on_device(tokens, hidden_grad, gate_value, up_value, gate_weight, up_weight):
    gathered = lax.all_gather(tokens, "tp", axis=0, tiled=True)
    gate_full, up_full = (
        lax.all_gather(gate_weight, "dp", axis=0, tiled=True),
        lax.all_gather(up_weight, "dp", axis=0, tiled=True),
    )
    gate_float = gate_value.astype(jnp.float32)
    up_float = up_value.astype(jnp.float32)
    logistic = jax.nn.sigmoid(gate_float)
    upstream = hidden_grad.astype(jnp.float32)
    d_gate = (upstream * up_float * logistic * (1.0 + gate_float * (1.0 - logistic))).astype(
        jnp.bfloat16
    )
    d_up = (upstream * gate_float * logistic).astype(jnp.bfloat16)
    across = (((1,), (1,)), ((), ()))
    contract = (((0,), (0,)), ((), ()))
    input_grad = lax.psum_scatter(
        (
            lax.dot_general(d_gate, gate_full, across, preferred_element_type=jnp.float32)
            + lax.dot_general(d_up, up_full, across, preferred_element_type=jnp.float32)
        ).astype(jnp.bfloat16),
        "tp",
        scatter_dimension=0,
        tiled=True,
    )
    grads_both = jnp.concatenate([d_gate, d_up], axis=1)
    hidden_width = d_gate.shape[1]
    group_rows = gathered.shape[0]
    columns = lax.all_to_all(gathered, "dp", split_axis=1, concat_axis=0, tiled=True)
    initial = jnp.zeros((gate_weight.shape[0], 2 * hidden_width), jnp.float32)
    pieces = lax.all_gather(grads_both, "dp", axis=0, tiled=True)
    group_count = pieces.shape[0] // group_rows

    def one_group(position, carried):
        within = position * group_rows
        grads_rows = lax.dynamic_slice_in_dim(pieces, within, group_rows, 0)
        block = lax.dynamic_slice_in_dim(columns, within, group_rows, 0)
        partial_value = lax.dot_general(
            block, grads_rows, contract, preferred_element_type=jnp.float32
        ).astype(jnp.bfloat16)
        partial_value = lax.optimization_barrier(partial_value)
        return carried + partial_value.astype(jnp.float32)

    summed = lax.fori_loop(0, group_count, one_group, initial)
    gate_grad = summed[:, :hidden_width].astype(jnp.bfloat16)
    up_grad = summed[:, hidden_width:].astype(jnp.bfloat16)
    return (input_grad, gate_grad, up_grad)


def solution(mesh):
    placed = (
        P(("dp", "tp"), None),
        P("dp", "tp"),
        P("dp", "tp"),
        P("dp", "tp"),
        P("dp", "tp"),
        P("dp", "tp"),
    )
    return jax.shard_map(
        on_device,
        mesh=mesh,
        in_specs=placed,
        out_specs=(P(("dp", "tp"), None), P("dp", "tp"), P("dp", "tp")),
        check_vma=False,
    )
```

profile of v0, /device:TPU:0, one launch (start us, length us, event | category | flops | bytes accessed | tf_op | source)
XLA Modules:
  0.0 376.7 jit_solution(9638341866954031148)
XLA Ops:
  7.2 0.7 all-gather.9.cloned.1.call-update
  8.0 0.7 all-gather.5.cloned.1.call-update
  9.5 1.8 fusion.12
  11.3 1.2 pad_maximum_fusion
  12.5 44.6 %all-gather.9.cloned.1.call-done = bf16[192,4096]{1,0:T(8,128)(2,1)} async-done(((bf16[24,4096]{1,0:T(8,128)(2,1)}), bf16[192,4096]{1,0:T(8,128)(2,1)}) %all-gather.9.cloned.1.call-update) | async-done | bytes 1572880 | tf_op jit(solution)/shard_map/all_gather | solution.py:8
  57.1 2.7 copy.12
  59.8 3.6 all-to-all-start
  63.4 100.7 %all-gather.5.cloned.1.call-done = bf16[4096,1792]{1,0:T(8,128)(2,1)} async-done(((bf16[1024,1792]{1,0:T(8,128)(2,1)}), bf16[4096,1792]{1,0:T(8,128)(2,1)}) %all-gather.5.cloned.1.call-update) | async-done | bytes 14680080 | tf_op jit(solution)/shard_map/all_gather | solution.py:10
  164.1 11.9 %fusion.14 = f32[192,4096]{1,0:T(8,128)} fusion(bf16[192,1792]{1,0:T(8,128)(2,1)S(1)} %get-tuple-element.109, bf16[4096,1792]{1,0:T(8,128)(2,1)} %all-gather.5.cloned.1.call-done), kind=kOutput, calls=%fused_computation.23 | convolution fusion | flops 2818572288 | bytes 18513920 | tf_op jit(solution)/shard_map/dot_general | solution.py:25
  176.0 81.2 %all-gather.7.cloned.1.call-done = bf16[4096,1792]{1,0:T(8,128)(2,1)} async-done(((bf16[1024,1792]{1,0:T(8,128)(2,1)}), bf16[4096,1792]{1,0:T(8,128)(2,1)}) %all-gather.7.cloned.1.call-update) | async-done | bytes 14680080 | tf_op jit(solution)/shard_map/all_gather | solution.py:11
  257.1 12.1 %fusion.3 = bf16[192,4096]{1,0:T(8,128)(2,1)} fusion(f32[192,4096]{1,0:T(8,128)} %fusion.14, bf16[192,1792]{1,0:T(8,128)(2,1)S(1)} %get-tuple-element.108, bf16[4096,1792]{1,0:T(8,128)(2,1)} %all-gather.7.cloned.1.call-done), kind=kOutput, calls=%fused_computation.6 | convolution fusion | flops 2820145152 | bytes 20086784 | tf_op jit(solution)/shard_map/dot_general | solution.py:26
  269.3 31.2 %all-gather.11.cloned.1.call-done = bf16[768,3584]{1,0:T(8,128)(2,1)} async-done(((bf16[192,3584]{1,0:T(8,128)(2,1)}), bf16[768,3584]{1,0:T(8,128)(2,1)}) %all-gather.11.cloned.1.call-update) | async-done | bytes 5505040 | tf_op jit(solution)/shard_map/all_gather | solution.py:37
  300.5 52.8 %while.14 = (s32[]{:T(128)}, f32[1024,3584]{1,0:T(8,128)}, bf16[768,1024]{1,0:T(8,128)(2,1)S(1)}, bf16[768,3584]{1,0:T(8,128)(2,1)}, s32[]{:T(128)}, /*index=5*/s32[]{:T(128)}, s32[]{:T(128)}, s32[]{:T(128)}) while((s32[]{:T(128)}, f32[1024,3584]{1,0:T(8,128)}, bf16[768,1024]{1,0:T(8,128)(2,1)S(1)}, bf16[768,3584]{1,0:T(8,128)(2,1)}, ...), condition=%wide.region_2.0_spmd.clone, body=%wide.region_1.0_spmd.clone.sunk | while | flops 1423966208 | bytes 45810836 | solution.py:50
  300.5 3.5 convolution_convert_fusion.2
  304.0 5.9 %select_add_fusion.2 = f32[1024,3584]{1,0:T(8,128)} fusion(f32[1024,3584]{1,0:T(8,128)} %get-tuple-element.144, bf16[1024,3584]{1,0:T(8,128)(2,1)S(1)} %convolution_convert_fusion.2, pred[]{:T(512)S(6)} %compare.3), kind=kLoop, calls=%fused_computation.clone.1 | loop fusion | flops 11010048 | bytes 36700160 | tf_op jit(solution)/shard_map/while/body/eval_jaxpr/add | solution.py:48
  309.9 3.4 convolution_convert_fusion.2
  313.4 11.0 %select_add_fusion.2 = f32[1024,3584]{1,0:T(8,128)} fusion(f32[1024,3584]{1,0:T(8,128)} %get-tuple-element.144, bf16[1024,3584]{1,0:T(8,128)(2,1)S(1)} %convolution_convert_fusion.2, pred[]{:T(512)S(6)} %compare.3), kind=kLoop, calls=%fused_computation.clone.1 | loop fusion | flops 11010048 | bytes 36700160 | tf_op jit(solution)/shard_map/while/body/eval_jaxpr/add | solution.py:48
  324.4 3.5 convolution_convert_fusion.2
  327.9 11.0 %select_add_fusion.2 = f32[1024,3584]{1,0:T(8,128)} fusion(f32[1024,3584]{1,0:T(8,128)} %get-tuple-element.144, bf16[1024,3584]{1,0:T(8,128)(2,1)S(1)} %convolution_convert_fusion.2, pred[]{:T(512)S(6)} %compare.3), kind=kLoop, calls=%fused_computation.clone.1 | loop fusion | flops 11010048 | bytes 36700160 | tf_op jit(solution)/shard_map/while/body/eval_jaxpr/add | solution.py:48
  338.9 3.4 convolution_convert_fusion.2
  342.3 11.0 %select_add_fusion.2 = f32[1024,3584]{1,0:T(8,128)} fusion(f32[1024,3584]{1,0:T(8,128)} %get-tuple-element.144, bf16[1024,3584]{1,0:T(8,128)(2,1)S(1)} %convolution_convert_fusion.2, pred[]{:T(512)S(6)} %compare.3), kind=kLoop, calls=%fused_computation.clone.1 | loop fusion | flops 11010048 | bytes 36700160 | tf_op jit(solution)/shard_map/while/body/eval_jaxpr/add | solution.py:48
  353.3 9.1 %convert.4 = bf16[1024,3584]{1,0:T(8,128)(2,1)} convert(f32[1024,3584]{1,0:T(8,128)} %get-tuple-element.82) | non-fusion elementwise | flops 3670016 | bytes 22020096 | tf_op jit(solution)/shard_map/convert.1
  362.4 6.7 %fusion.13 = (bf16[1024,1792]{1,0:T(8,128)(2,1)}, bf16[1024,1792]{1,0:T(8,128)(2,1)}) fusion(bf16[1024,3584]{1,0:T(8,128)(2,1)} %convert.4), kind=kLoop, calls=%fused_computation.22 | loop fusion | bytes 14680064 | tf_op jit(solution)/shard_map/slice | solution.py:52
  369.1 1.0 reduce-scatter.2.cloned.1.call-done
  (14 shorter events, 0.9 us)
Async XLA Ops:
  7.2 49.9 %all-gather.9.cloned.1.call-start = ((), (), s32[]{:S(2)}) async-start(), calls=%async_computation.5 | async-start | bytes 1769472 | tf_op jit(solution)/shard_map/all_gather | solution.py:8
  7.9 1.6 copy-start
  7.9 1.6 copy-start.1
  7.9 156.2 %all-gather.5.cloned.1.call-start = ((), (), s32[]{:S(2)}) async-start(), calls=%async_computation.2 | async-start | bytes 18350080 | tf_op jit(solution)/shard_map/all_gather | solution.py:10
  8.7 248.5 %all-gather.7.cloned.1.call-start = ((), (), s32[]{:S(2)}) async-start(), calls=%async_computation.3 | async-start | bytes 18350080 | tf_op jit(solution)/shard_map/all_gather | solution.py:11
  9.4 291.1 %all-gather.11.cloned.1.call-start = ((), (), s32[]{:S(2)}) async-start(), calls=%async_computation.6 | async-start | bytes 6881280 | tf_op jit(solution)/shard_map/all_gather | solution.py:37
  59.8 209.5 %all-to-all-start = ((bf16[192,4,1024]{2,0,1:T(8,128)(2,1)}), bf16[192,4,1024]{2,0,1:T(8,128)(2,1)S(1)}, u32[]{:S(2)}, u32[]{:S(2)}) async-start(bf16[192,4,1024]{2,0,1:T(8,128)(2,1)} %bitcast.10), calls=%async_computation.1 | async-start | bytes 3145728 | tf_op jit(solution)/shard_map/all_to_all | solution.py:35
  63.4 306.8 %reduce-scatter.2.cloned.1.call-start = ((), (), s32[]{:S(2)}) async-start(), calls=%async_computation.4 | async-start | bytes 1769472 | tf_op jit(solution)/shard_map/reduce_scatter | solution.py:23
Sparse Core Ops, SparseCore 0:
  10.2 46.8 all-gather.8
  58.6 105.4 all-gather.4
  165.7 91.4 all-gather.6
  258.6 41.8 all-gather.10
  304.3 65.7 reduce-scatter.1
where the time goes:
time: 377 us
  waiting for transfers between devices  261 us (69%)
  other arithmetic  51.1 us (14%)
  matrix products  37.9 us (10%)
  between operations  13.8 us (4%)
  local copies, waits for them, and re-layouts  9.4 us (2%)
    all_gather x1, waiting for transfers between devices, on_device(): lax.all_gather(gate_weight, 'dp', axis=0, tiled=True)  101 us
    all_gather x1, waiting for transfers between devices, on_device(): lax.all_gather(up_weight, 'dp', axis=0, tiled=True)  81.2 us
    all_gather x1, waiting for transfers between devices, on_device(): gathered = lax.all_gather(tokens, 'tp', axis=0, tiled=True)  44.6 us
    add x4, other arithmetic, one_group(): return carried + partial_value.astype(jnp.float32)  39 us
    all_gather x1, waiting for transfers between devices, on_device(): pieces = lax.all_gather(grads_both, 'dp', axis=0, tiled=True)  31.2 us
    dot_general x4, matrix products, one_group(): lax.dot_general(block, grads_rows, contract, preferred_element_type=jnp.f...  13.8 us
    dot_general x1, matrix products, on_device(): lax.dot_general(d_up, up_full, across, preferred_element_type=jnp.float32)  12.1 us
    dot_general x1, matrix products, on_device(): lax.dot_general(d_gate, gate_full, across, preferred_element_type=jnp.flo...  11.9 us
  transfers between devices with their start and end apart: 6, of which 5 were waited for; matrix products, arithmetic and copies ran while one was open for 26% of the time, Pallas kernels for 0%

commit v1 on v0

v1 whole, which is shorter than its diff:
```python
import jax
import jax.numpy as jnp
from jax import lax
from jax.sharding import PartitionSpec as P


def on_device(tokens, hidden_grad, gate_value, up_value, gate_weight, up_weight):
    n_dp = lax.axis_size("dp")
    n_tp = lax.axis_size("tp")
    token_rows, features = tokens.shape
    width = gate_weight.shape[0]
    hidden_width = gate_value.shape[1]

    gate_float = gate_value.astype(jnp.float32)
    up_float = up_value.astype(jnp.float32)
    logistic = jax.nn.sigmoid(gate_float)
    upstream = hidden_grad.astype(jnp.float32)
    d_gate = (upstream * up_float * logistic * (1.0 + gate_float * (1.0 - logistic))).astype(
        jnp.bfloat16
    )
    d_up = (upstream * gate_float * logistic).astype(jnp.bfloat16)
    pieces = lax.all_gather(jnp.concatenate([d_gate, d_up], axis=1), "dp", axis=0, tiled=True)

    mine = lax.all_to_all(tokens, "dp", split_axis=1, concat_axis=0, tiled=True)
    columns = lax.all_gather(mine, "tp", axis=0, tiled=True)
    columns = columns.reshape(n_tp, n_dp, token_rows, width).transpose(1, 0, 2, 3)
    columns = columns.reshape(n_tp * n_dp * token_rows, width)

    across = (((1,), (1,)), ((), ()))
    contract = (((0,), (0,)), ((), ()))
    partial = (
        lax.dot_general(
            pieces[:, :hidden_width], gate_weight, across, preferred_element_type=jnp.float32
        )
        + lax.dot_general(
            pieces[:, hidden_width:], up_weight, across, preferred_element_type=jnp.float32
        )
    ).astype(jnp.bfloat16)
    partial = partial.reshape(n_dp, n_tp, token_rows, width).transpose(1, 0, 2, 3)
    partial = partial.reshape(n_tp * n_dp * token_rows, width)
    summed = lax.psum_scatter(partial, "tp", scatter_dimension=0, tiled=True)
    input_grad = lax.all_to_all(summed, "dp", split_axis=0, concat_axis=1, tiled=True)

    gate_grad = lax.dot_general(
        columns, pieces[:, :hidden_width], contract, preferred_element_type=jnp.float32
    ).astype(jnp.bfloat16)
    up_grad = lax.dot_general(
        columns, pieces[:, hidden_width:], contract, preferred_element_type=jnp.float32
    ).astype(jnp.bfloat16)
    return (input_grad, gate_grad, up_grad)


def solution(mesh):
    placed = (
        P(("dp", "tp"), None),
        P("dp", "tp"),
        P("dp", "tp"),
        P("dp", "tp"),
        P("dp", "tp"),
        P("dp", "tp"),
    )
    return jax.shard_map(
        on_device,
        mesh=mesh,
        in_specs=placed,
        out_specs=(P(("dp", "tp"), None), P("dp", "tp"), P("dp", "tp")),
        check_vma=False,
    )
```

time: 377 us -> 199 us (0.53)
  waiting for transfers between devices: 261 us -> 131 us
  other arithmetic: 51.1 us -> 3.4 us
  matrix products: 37.9 us -> 21.8 us
  blocking collectives: 0 us -> 9.44 us
  local copies, waits for them, and re-layouts: 9.4 us -> 15.4 us
    all_gather x4 -> x2, waiting for transfers between devices: 258 us -> 71.2 us  [the longest x1 36 us: on_device(): columns = lax.all_gather(mine, 'tp', axis=0, tiled=True)]
    reduce_scatter x1, waiting for transfers between devices: 1.01 us -> 60 us  [on_device(): summed = lax.psum_scatter(partial, 'tp', scatter_dimension=0, tiled=True)]
    add x4 -> x0, other arithmetic: 39 us -> none  [one_group(): return carried + partial_value.astype(jnp.float32)]
    dot_general x6 -> x4, matrix products: 37.9 us -> 21.8 us  [the longest x1 6.42 us: on_device(): lax.dot_general(columns, pieces[:, :hidden_width], contract, preferred_el...]
    unnamed x4 -> x8, local copies, waits for them, and re-layouts: 0.01 us -> 11.8 us
    all_to_all x0 -> x1, blocking collectives: none -> 9.44 us  [on_device(): mine = lax.all_to_all(tokens, 'dp', split_axis=1, concat_axis=0, tiled=True)]
    another operation x1 -> x0, other arithmetic: 9.12 us -> none
    slice x1 -> x0, local copies, waits for them, and re-layouts: 6.69 us -> none  [on_device(): up_grad = summed[:, hidden_width:].astype(jnp.bfloat16)]
  transfers between devices with their start and end apart: 6 -> 4, of which waited for: 5 -> 3; matrix products, arithmetic and copies ran while one was open for 26% -> 18% of each run, Pallas kernels for 0% -> 0%
where the time goes in v1:
time: 199 us; the launch traced here: 198 us
  waiting for transfers between devices  131 us (66%)
  matrix products  21.8 us (11%)
  local copies, waits for them, and re-layouts  15.4 us (8%)
  between operations  13.8 us (7%)
  blocking collectives  9.44 us (5%)
  starting transfers between devices  3.49 us (2%)
  other arithmetic  3.4 us (2%)
    reduce_scatter x1, waiting for transfers between devices, on_device(): summed = lax.psum_scatter(partial, 'tp', scatter_dimension=0, tiled=True)  60 us
    all_gather x1, waiting for transfers between devices, on_device(): columns = lax.all_gather(mine, 'tp', axis=0, tiled=True)  36 us
    all_gather x1, waiting for transfers between devices, on_device(): lax.all_gather(jnp.concatenate([d_gate, d_up], axis=1), 'dp', axis=0, til...  35.2 us
    unnamed x8, local copies, waits for them, and re-layouts  11.8 us
    all_to_all x1, blocking collectives, on_device(): mine = lax.all_to_all(tokens, 'dp', split_axis=1, concat_axis=0, tiled=True)  9.44 us
    dot_general x1, matrix products, on_device(): lax.dot_general(columns, pieces[:, :hidden_width], contract, preferred_el...  6.42 us
    dot_general x1, matrix products, on_device(): lax.dot_general(columns, pieces[:, hidden_width:], contract, preferred_el...  6.3 us
    dot_general x1, matrix products, on_device(): lax.dot_general(pieces[:, hidden_width:], up_weight, across, preferred_el...  6.04 us
  transfers between devices with their start and end apart: 4, of which 3 were waited for; matrix products, arithmetic and copies ran while one was open for 18% of the time, Pallas kernels for 0%

profile of v1, /device:TPU:0, one launch (start us, length us, event | category | flops | bytes accessed | tf_op | source)
XLA Modules:
  0.0 198.5 jit_solution(8815059297840828324)
XLA Ops:
  7.2 0.0 all-gather.3.cloned.1.call-start
  7.2 2.2 %fusion.12 = (bf16[192,1792]{1,0:T(8,128)(2,1)S(1)}, bf16[192,1792]{1,0:T(8,128)(2,1)S(1)}) fusion(bf16[192,1792]{1,0:T(8,128)(2,1)} %param.7, bf16[192,1792]{1,0:T(8,128)(2,1)} %param.8, bf16[192,1792]{1,0:T(8,128)(2,1)} %param.9), kind=kLoop, calls=%fused_computation.17 | loop fusion | flops 5505024 | bytes 3440640 | tf_op jit(solution)/shard_map/convert_element_type | solution.py:18
  9.4 0.0 copy-start
  9.5 1.2 pad_maximum_fusion
  10.6 0.0 all-gather.3.cloned.1.call-update
  10.6 0.0 all-gather.5.cloned.1.call-start
  10.7 9.4 %all_to_all.38 = bf16[24,4,1024]{2,0,1:T(8,128)(2,1)} all-to-all(bf16[24,4,1024]{2,0,1:T(8,128)(2,1)S(1)} %bitcast.34), channel_id=1, replica_groups=mesh['tp'=8,'dp'=4] {'dp'}, dimensions={1} | all-to-all | bytes 393216 | tf_op jit(solution)/shard_map/all_to_all | solution.py:24
  20.2 0.0 all-gather.5.cloned.1.call-update
  20.2 0.0 reduce-scatter.2.cloned.1.call-start
  20.2 35.2 %all-gather.3.cloned.1.call-done = bf16[768,3584]{1,0:T(8,128)(2,1)} async-done(((bf16[192,3584]{1,0:T(8,128)(2,1)}), bf16[768,3584]{1,0:T(8,128)(2,1)}) %all-gather.3.cloned.1.call-update) | async-done | bytes 5505040 | tf_op jit(solution)/shard_map/all_gather | solution.py:22
  55.4 6.0 %fusion.3 = f32[768,1024]{1,0:T(8,128)S(1)} fusion(bf16[1024,1792]{1,0:T(8,128)(2,1)} %param.11, bf16[768,3584]{1,0:T(8,128)(2,1)} %all-gather.3.cloned.1.call-done), kind=kOutput, calls=%fused_computation.6 | convolution fusion | flops 2818572288 | bytes 9568256 | tf_op jit(solution)/shard_map/dot_general | solution.py:35
  61.5 3.0 %add_convert_fusion = bf16[768,1024]{1,0:T(8,128)(2,1)S(1)} fusion(f32[768,1024]{1,0:T(8,128)S(1)} %fusion.3, bf16[1024,1792]{1,0:T(8,128)(2,1)S(1)} %copy-done.2, bf16[768,3584]{1,0:T(8,128)(2,1)S(1)} %copy-done.1), kind=kOutput, calls=%fused_computation.4 | convolution fusion | flops 2820145152 | bytes 11141120 | tf_op jit(solution)/shard_map/dot_general | solution.py:32
  64.5 1.3 copy.21
  65.8 0.0 reduce-scatter.2.cloned.1.call-update
  65.8 36.0 %all-gather.5.cloned.1.call-done = bf16[768,1024]{1,0:T(8,128)(2,1)} async-done(((bf16[96,1024]{1,0:T(8,128)(2,1)}), bf16[768,1024]{1,0:T(8,128)(2,1)}) %all-gather.5.cloned.1.call-update) | async-done | bytes 1572880 | tf_op jit(solution)/shard_map/all_gather | solution.py:25
  101.8 1.6 copy.24
  103.4 6.4 %fusion = bf16[1024,1792]{0,1:T(8,128)(2,1)} fusion(bf16[768,1024]{1,0:T(8,128)(2,1)S(1)} %bitcast.29, bf16[768,3584]{1,0:T(8,128)(2,1)} %all-gather.3.cloned.1.call-done), kind=kOutput, calls=%fused_computation.2 | convolution fusion | flops 2820407296 | bytes 7995392 | tf_op jit(solution)/shard_map/dot_general | solution.py:44
  109.8 60.0 %reduce-scatter.2.cloned.1.call-done = bf16[96,1024]{1,0:T(8,128)(2,1)} async-done(((bf16[768,1024]{1,0:T(8,128)(2,1)}), bf16[96,1024]{1,0:T(8,128)(2,1)}) %reduce-scatter.2.cloned.1.call-update) | async-done | bytes 196624 | tf_op jit(solution)/shard_map/reduce_scatter | solution.py:41
  169.8 3.4 %all-to-all-start = ((bf16[4,24,1024]{2,1,0:T(8,128)(2,1)}), bf16[4,24,1024]{2,1,0:T(8,128)(2,1)S(1)}, u32[]{:S(2)}, u32[]{:S(2)}) async-start(bf16[4,24,1024]{2,1,0:T(8,128)(2,1)} %bitcast.36), calls=%async_computation.1 | async-start | bytes 393216 | tf_op jit(solution)/shard_map/all_to_all | solution.py:42
  173.1 6.3 %fusion.1 = bf16[1024,1792]{0,1:T(8,128)(2,1)} fusion(bf16[768,1024]{1,0:T(8,128)(2,1)S(1)} %bitcast.30, bf16[768,3584]{1,0:T(8,128)(2,1)} %all-gather.3.cloned.1.call-done), kind=kOutput, calls=%fused_computation.3 | convolution fusion | flops 2820407296 | bytes 7995392 | tf_op jit(solution)/shard_map/dot_general | solution.py:47
  179.4 5.9 %copy.26 = bf16[1024,1792]{1,0:T(8,128)(2,1)} copy(bf16[1024,1792]{0,1:T(8,128)(2,1)} %fusion.1) | data formatting | bytes 7340032
  185.3 5.9 %copy.25 = bf16[1024,1792]{1,0:T(8,128)(2,1)} copy(bf16[1024,1792]{0,1:T(8,128)(2,1)} %fusion) | data formatting | bytes 7340032
  191.3 0.0 all-to-all-done
  191.3 0.7 copy.28
  (6 shorter events, 0.0 us)
Async XLA Ops:
  7.2 48.3 %all-gather.3.cloned.1.call-start = ((), (), s32[]{:S(2)}) async-start(), calls=%async_computation.3 | async-start | bytes 6881280 | tf_op jit(solution)/shard_map/all_gather | solution.py:22
  9.4 1.3 copy-start
  10.6 91.2 %all-gather.5.cloned.1.call-start = ((), (), s32[]{:S(2)}) async-start(), calls=%async_computation.5 | async-start | bytes 1769472 | tf_op jit(solution)/shard_map/all_gather | solution.py:25
  20.2 149.6 %reduce-scatter.2.cloned.1.call-start = ((), (), s32[]{:S(2)}) async-start(), calls=%async_computation.4 | async-start | bytes 1769472 | tf_op jit(solution)/shard_map/reduce_scatter | solution.py:41
  55.4 6.1 %copy-start.1 = (bf16[768,3584]{1,0:T(8,128)(2,1)S(1)}, bf16[768,3584]{1,0:T(8,128)(2,1)}, u32[]{:S(2)}) copy-start(bf16[768,3584]{1,0:T(8,128)(2,1)} %all-gather.3.cloned.1.call-done) | copy-start | bytes 16515076
  55.4 6.1 %copy-start.2 = (bf16[1024,1792]{1,0:T(8,128)(2,1)S(1)}, bf16[1024,1792]{1,0:T(8,128)(2,1)}, u32[]{:S(2)}) copy-start(bf16[1024,1792]{1,0:T(8,128)(2,1)} %param.10) | copy-start | bytes 11010052
  169.8 21.5 %all-to-all-start = ((bf16[4,24,1024]{2,1,0:T(8,128)(2,1)}), bf16[4,24,1024]{2,1,0:T(8,128)(2,1)S(1)}, u32[]{:S(2)}, u32[]{:S(2)}) async-start(bf16[4,24,1024]{2,1,0:T(8,128)(2,1)} %bitcast.36), calls=%async_computation.1 | async-start | bytes 393216 | tf_op jit(solution)/shard_map/all_to_all | solution.py:42
Sparse Core Ops, SparseCore 0:
  10.8 44.6 all-gather.2
  57.6 44.1 all-gather.4
  105.8 63.8 reduce-scatter.1

commit v2 on v1

v2 whole, which is shorter than its diff:
```python
import functools

import jax
import jax.numpy as jnp
from jax import lax
from jax.experimental import pallas as pl
from jax.experimental.pallas import tpu as pltpu
from jax.sharding import PartitionSpec as P

MESH = pl.DeviceIdType.MESH
ACROSS = (((1,), (1,)), ((), ()))
CONTRACT = (((0,), (0,)), ((), ()))


def exchange(
    n_dp,
    n_tp,
    outer,
    inner,
    tokens_ref,
    hidden_ref,
    gate_ref,
    up_ref,
    gate_weight_hbm,
    up_weight_hbm,
    input_grad_ref,
    grads_hbm,
    columns_hbm,
    grads,
    columns,
    gate_weight,
    up_weight,
    part,
    inner_got,
    outer_send,
    outer_got,
    final,
    placed,
    local_sem,
    token_sem,
    token_outer_sem,
    token_inner_sem,
    pair_sem,
    chip_sem,
    relay_sem,
    inner_sem,
    outer_sem,
    final_sem,
    store_sem,
):
    token_rows = tokens_ref.shape[0]
    width = gate_weight.shape[0]
    hidden = gate_weight.shape[1]
    group_rows = n_tp * token_rows
    chunk_rows = inner * token_rows
    chips = n_dp // 2

    dp = lax.axis_index("dp")
    tp = lax.axis_index("tp")
    chip, core = lax.div(dp, 2), lax.rem(dp, 2)
    far, near = lax.div(tp, inner), lax.rem(tp, inner)

    def pair_device():
        return {"dp": chip * 2 + (1 - core)}

    def chip_device(offset):
        return {"dp": lax.rem(chip + offset, chips) * 2 + core}

    def dp_device(offset):
        return {"dp": lax.rem(dp + offset, n_dp)}

    def outer_device(offset):
        return {"tp": lax.rem(far + offset, outer) * inner + near}

    def inner_device(offset):
        return {"tp": far * inner + lax.rem(near + offset, inner)}

    sends = []

    def send(source, target, sems, index, device):
        copy = pltpu.make_async_remote_copy(
            src_ref=source,
            dst_ref=target,
            send_sem=sems.at[(0, *index)],
            recv_sem=sems.at[(1, *index)],
            device_id=device,
            device_id_type=MESH,
        )
        copy.start()
        sends.append(copy)
        return copy

    weight_copies = [
        pltpu.make_async_copy(gate_weight_hbm, gate_weight, local_sem.at[0]),
        pltpu.make_async_copy(up_weight_hbm, up_weight, local_sem.at[1]),
    ]
    for copy in weight_copies:
        copy.start()

    barrier = pltpu.get_barrier_semaphore()
    peers = (
        [dp_device(offset) for offset in range(1, n_dp)]
        + [outer_device(offset) for offset in range(1, outer)]
        + [inner_device(offset) for offset in range(1, inner)]
    )
    for peer in peers:
        pl.semaphore_signal(barrier, inc=1, device_id=peer, device_id_type=MESH)
    pl.semaphore_wait(barrier, len(peers))

    token_copies = []
    for offset in range(1, n_dp):
        start = pl.multiple_of(lax.rem(dp + offset, n_dp) * width, width)
        token_copies.append(
            send(
                tokens_ref.at[:, pl.ds(start, width)],
                columns.at[dp, tp],
                token_sem,
                (offset - 1,),
                dp_device(offset),
            )
        )
    own_columns = pltpu.make_async_copy(
        tokens_ref.at[:, pl.ds(pl.multiple_of(dp * width, width), width)],
        columns.at[dp, tp],
        local_sem.at[2],
    )
    own_columns.start()

    block = 256 if hidden % 256 == 0 else 128
    step_rows = 16

    def chunk_at(k):
        return lax.rem(far + k, outer)

    def rows_of(k):
        return pl.ds(pl.multiple_of(chunk_at(k) * chunk_rows, chunk_rows), chunk_rows)

    def form_chunk(k):
        base = chunk_at(k) * chunk_rows

        def form(step, carry):
            rows = pl.ds(pl.multiple_of(base + step * step_rows, step_rows), step_rows)
            for column in range(0, hidden, block):
                there = pl.ds(column, block)
                g = gate_ref[rows, there].astype(jnp.float32)
                u = up_ref[rows, there].astype(jnp.float32)
                h = hidden_ref[rows, there].astype(jnp.float32)
                s = 1.0 / (1.0 + jnp.exp(-g))
                hs = h * s
                grads[dp, rows, there] = (hs * u * (1.0 + g * (1.0 - s))).astype(jnp.bfloat16)
                grads[dp, rows, pl.ds(hidden + column, block)] = (hs * g).astype(jnp.bfloat16)
            return carry

        lax.fori_loop(0, chunk_rows // step_rows, form, 0)

    pair_copies, chip_copies = [], {}

    def send_chunk(k):
        rows = rows_of(k)
        for offset in range(1, chips):
            chip_copies[offset, k] = send(
                grads.at[dp, rows],
                grads.at[dp, rows],
                chip_sem,
                (offset - 1, k),
                chip_device(offset),
            )
        pair_copies.append(
            send(grads.at[dp, rows], grads.at[dp, rows], pair_sem, (k,), pair_device())
        )

    for k in range(outer):
        form_chunk(k)
        if k >= 1:
            send_chunk(k - 1)
    own_columns.wait()
    for copy in token_copies:
        copy.wait_recv()
    send_chunk(outer - 1)

    token_outer = [
        send(
            columns.at[:, tp],
            columns.at[:, tp],
            token_outer_sem,
            (offset - 1,),
            outer_device(offset),
        )
        for offset in range(1, outer)
    ]

    tile = 256 if width % 256 == 0 else 128

    def project(first, chunk):
        def one_tile(n, carry):
            there = pl.ds(pl.multiple_of(n * tile, tile), tile)
            if chunk is None:
                rows, count = slice(None), group_rows
            else:
                rows = pl.ds(pl.multiple_of(chunk * chunk_rows, chunk_rows), chunk_rows)
                count = chunk_rows
            d_gate = grads[pl.ds(first, 2), rows, pl.ds(0, hidden)].reshape(2 * count, hidden)
            d_up = grads[pl.ds(first, 2), rows, pl.ds(hidden, hidden)].reshape(2 * count, hidden)
            total = lax.dot_general(
                d_gate, gate_weight[there, :], ACROSS, preferred_element_type=jnp.float32
            ) + lax.dot_general(
                d_up, up_weight[there, :], ACROSS, preferred_element_type=jnp.float32
            )
            for row in range(0, 2 * count, token_rows):
                group, within = divmod(row, count)
                at, to = divmod(within // token_rows, inner)
                at = at if chunk is None else chunk
                part[first + group, at, to, :, there] = total[row : row + token_rows].astype(
                    jnp.bfloat16
                )
            return carry

        lax.fori_loop(0, width // tile, one_tile, 0)

    def send_inner(first, chip_index, k):
        at = chunk_at(k)
        return [
            send(
                part.at[pl.ds(first, 2), at, lax.rem(near + offset, inner)],
                inner_got.at[offset - 1, pl.ds(first, 2), at],
                inner_sem,
                (chip_index, k, offset - 1),
                inner_device(offset),
            )
            for offset in range(1, inner)
        ]

    outer_copies = {}

    def add_inner(first, chip_index, k, copies):
        at = chunk_at(k)
        for copy in copies:
            copy.wait_recv()
        for group in range(2):
            total = part[first + group, at, near].astype(jnp.float32)
            for offset in range(1, inner):
                total = total + inner_got[offset - 1, first + group, at].astype(jnp.float32)
            outer_send[first + group, k] = total.astype(jnp.bfloat16)
        if k > 0:
            outer_copies[chip_index, k] = send(
                outer_send.at[pl.ds(first, 2), k],
                outer_got.at[k - 1, pl.ds(first, 2)],
                outer_sem,
                (chip_index, k - 1),
                outer_device(k),
            )

    own_first = chip * 2
    for copy in pair_copies:
        copy.wait_recv()
    for copy in weight_copies:
        copy.wait()
    stores = []

    def store(source, target, index):
        copy = pltpu.make_async_copy(source, target, store_sem.at[index])
        copy.start()
        stores.append(copy)

    store(grads.at[pl.ds(own_first, 2)], grads_hbm.at[pl.ds(own_first, 2)], 0)
    project(own_first, None)
    order = list(range(1, outer)) + [0]
    own_inner = {k: send_inner(own_first, 0, k) for k in order}

    token_inner = []

    def spread_tokens(k):
        source = lax.rem(far - k + outer, outer) * inner + near
        for offset in range(1, inner):
            token_inner.append(
                send(
                    columns.at[:, source],
                    columns.at[:, source],
                    token_inner_sem,
                    (k, offset - 1),
                    inner_device(offset),
                )
            )

    spread_tokens(0)
    for k in order:
        add_inner(own_first, 0, k, own_inner[k])
    for k in range(1, outer):
        token_outer[k - 1].wait_recv()
        spread_tokens(k)

    waiting = []
    for k in range(outer):
        relays = []
        for offset in range(1, chips):
            chip_copies[offset, k].wait_recv()
            source = lax.rem(chip - offset + chips, chips) * 2 + core
            relays.append(
                send(
                    grads.at[source, rows_of(k)],
                    grads.at[source, rows_of(k)],
                    relay_sem,
                    (offset - 1, k),
                    pair_device(),
                )
            )
        for offset in range(1, chips):
            relays[offset - 1].wait_recv()
            first = lax.rem(chip - offset + chips, chips) * 2
            store(
                grads.at[pl.ds(first, 2), rows_of(k)],
                grads_hbm.at[pl.ds(first, 2), rows_of(k)],
                1 + (offset - 1) * outer + k,
            )
            project(first, chunk_at(k))
            waiting.append((first, offset, k, send_inner(first, offset, k)))
            if len(waiting) > 1:
                add_inner(*waiting.pop(0))
    while waiting:
        add_inner(*waiting.pop(0))

    for copy in token_inner:
        copy.wait_recv()
    store(columns, columns_hbm, 1 + max(chips - 1, 0) * outer)

    finals = {}
    for index in range(chips):
        first = lax.rem(chip - index + chips, chips) * 2
        for k in range(1, outer):
            outer_copies[index, k].wait_recv()
        for group in range(2):
            total = outer_send[first + group, 0].astype(jnp.float32)
            for k in range(1, outer):
                total = total + outer_got[k - 1, first + group].astype(jnp.float32)
            final[first + group] = total.astype(jnp.bfloat16)
        if index > 0:
            for turn in range(2):
                group = first + lax.rem(core + turn, 2)
                finals[index, turn] = send(
                    final.at[group],
                    placed.at[dp],
                    final_sem,
                    (index, turn),
                    {"dp": group},
                )
        else:
            finals[0, 1] = send(
                final.at[first + 1 - core], placed.at[dp], final_sem, (0, 1), pair_device()
            )
    placed[dp] = final[dp]
    for copy in finals.values():
        copy.wait_recv()
    for source in range(n_dp):
        input_grad_ref[:, source * width : (source + 1) * width] = placed[source]

    for copy in sends:
        copy.wait_send()
    for copy in stores:
        copy.wait()


def on_device(n_dp, n_tp, tokens, hidden_grad, gate_value, up_value, gate_weight, up_weight):
    token_rows, features = tokens.shape
    width, hidden = gate_weight.shape
    inner = 2 if n_tp % 2 == 0 else 1
    outer = n_tp // inner
    chips = n_dp // 2
    group_rows = n_tp * token_rows
    bf16 = jnp.bfloat16
    dma = pltpu.SemaphoreType.DMA
    vmem = pl.BlockSpec(memory_space=pltpu.VMEM)
    hbm = pl.BlockSpec(memory_space=pl.ANY)
    others = max(chips - 1, 1)
    input_grad, grads, columns = pl.pallas_call(
        functools.partial(exchange, n_dp, n_tp, outer, inner),
        out_shape=(
            jax.ShapeDtypeStruct((token_rows, features), bf16),
            jax.ShapeDtypeStruct((n_dp, group_rows, 2 * hidden), bf16),
            jax.ShapeDtypeStruct((n_dp, n_tp, token_rows, width), bf16),
        ),
        in_specs=[vmem, vmem, vmem, vmem, hbm, hbm],
        out_specs=(vmem, hbm, hbm),
        scratch_shapes=[
            pltpu.VMEM((n_dp, group_rows, 2 * hidden), bf16),
            pltpu.VMEM((n_dp, n_tp, token_rows, width), bf16),
            pltpu.VMEM((width, hidden), bf16),
            pltpu.VMEM((width, hidden), bf16),
            pltpu.VMEM((n_dp, outer, inner, token_rows, width), bf16),
            pltpu.VMEM((max(inner - 1, 1), n_dp, outer, token_rows, width), bf16),
            pltpu.VMEM((n_dp, outer, token_rows, width), bf16),
            pltpu.VMEM((max(outer - 1, 1), n_dp, token_rows, width), bf16),
            pltpu.VMEM((n_dp, token_rows, width), bf16),
            pltpu.VMEM((n_dp, token_rows, width), bf16),
            dma((3,)),
            dma((2, n_dp - 1)),
            dma((2, max(outer - 1, 1))),
            dma((2, outer, max(inner - 1, 1))),
            dma((2, outer)),
            dma((2, others, outer)),
            dma((2, others, outer)),
            dma((2, chips, outer, max(inner - 1, 1))),
            dma((2, chips, max(outer - 1, 1))),
            dma((2, chips, 2)),
            dma((2 + others * outer,)),
        ],
        compiler_params=pltpu.CompilerParams(
            collective_id=0, has_side_effects=True, vmem_limit_bytes=60 * 1024 * 1024
        ),
    )(tokens, hidden_grad, gate_value, up_value, gate_weight, up_weight)
    grads = grads.reshape(n_dp * group_rows, 2 * hidden)
    columns = columns.reshape(n_dp * group_rows, width)
    gate_grad = lax.dot_general(
        columns, grads[:, :hidden], CONTRACT, preferred_element_type=jnp.float32
    ).astype(bf16)
    up_grad = lax.dot_general(
        columns, grads[:, hidden:], CONTRACT, preferred_element_type=jnp.float32
    ).astype(bf16)
    return (input_grad, gate_grad, up_grad)


def solution(mesh):
    placed = (
        P(("dp", "tp"), None),
        P("dp", "tp"),
        P("dp", "tp"),
        P("dp", "tp"),
        P("dp", "tp"),
        P("dp", "tp"),
    )
    return jax.shard_map(
        functools.partial(on_device, mesh.shape["dp"], mesh.shape["tp"]),
        mesh=mesh,
        in_specs=placed,
        out_specs=(P(("dp", "tp"), None), P("dp", "tp"), P("dp", "tp")),
        check_vma=False,
    )
```

time: 199 us -> 79.2 us (0.40)
  waiting for transfers between devices: 131 us -> 0 us
  Pallas kernels: 0 us -> 65.9 us
  local copies, waits for them, and re-layouts: 15.4 us -> 0.69 us
  between operations: 13.8 us -> 0.66 us
  matrix products: 21.8 us -> 11.8 us
  blocking collectives: 9.44 us -> 0 us
  starting transfers between devices: 3.49 us -> 0 us
  other arithmetic: 3.4 us -> 0 us
    all_gather x2 -> x0, waiting for transfers between devices: 71.2 us -> none  [the longest x1 36 us: on_device(): columns = lax.all_gather(mine, 'tp', axis=0, tiled=True)]
    pallas_call x0 -> x1, Pallas kernels: none -> 65.9 us  [on_device(): pl.pallas_call(functools.partial(exchange, n_dp, n_tp, outer, inner), out...]
    reduce_scatter x1 -> x0, waiting for transfers between devices: 60 us -> none  [on_device(): summed = lax.psum_scatter(partial, 'tp', scatter_dimension=0, tiled=True)]
    unnamed x8 -> x7, local copies, waits for them, and re-layouts: 11.8 us -> 0.69 us
    dot_general x4 -> x2, matrix products: 21.8 us -> 11.8 us  [the longest x1 7.31 us: on_device(): lax.dot_general(columns, grads[:, hidden:], CONTRACT, preferred_element_t...]
    all_to_all x1 -> x0, blocking collectives: 9.44 us -> none  [on_device(): mine = lax.all_to_all(tokens, 'dp', split_axis=1, concat_axis=0, tiled=True)]
    all_to_all x1 -> x0, starting transfers between devices: 3.36 us -> none  [on_device(): lax.all_to_all(summed, 'dp', split_axis=0, concat_axis=1, tiled=True)]
    reshape x2 -> x0, local copies, waits for them, and re-layouts: 2.82 us -> none  [the longest x1 1.56 us: on_device(): columns.reshape(n_tp, n_dp, token_rows, width).transpose(1, 0, 2, 3)]
  transfers between devices with their start and end apart: 4 -> 0, of which waited for: 3 -> 0; matrix products, arithmetic and copies ran while one was open for 18% -> 0% of each run, Pallas kernels for 0% -> 0%
where the time goes in v2:
time: 79.2 us; the launch traced here: 79.1 us
  Pallas kernels  65.9 us (83%)
  matrix products  11.8 us (15%)
    pallas_call x1, Pallas kernels, on_device(): pl.pallas_call(functools.partial(exchange, n_dp, n_tp, outer, inner), out...  65.9 us
    dot_general x1, matrix products, on_device(): lax.dot_general(columns, grads[:, hidden:], CONTRACT, preferred_element_t...  7.31 us
    dot_general x1, matrix products, on_device(): lax.dot_general(columns, grads[:, :hidden], CONTRACT, preferred_element_t...  4.53 us

profile of v2, /device:TPU:0, one launch (start us, length us, event | category | flops | bytes accessed | tf_op | source)
XLA Modules:
  0.0 79.1 jit_solution(14128348208078134881)
XLA Ops:
  0.6 65.9 %shard_map.85 = (bf16[24,4096]{1,0:T(8,128)(2,1)}, bf16[4,192,3584]{2,1,0:T(8,128)(2,1)}, bf16[4,8,24,1024]{3,2,1,0:T(8,128)(2,1)}) custom-call(bf16[24,4096]{1,0:T(8,128)(2,1)} %tokens_ref.1, bf16[192,1792]{1,0:T(8,128)(2,1)} %hidden_ref.1, bf16[192,1792]{1,0:T(8,128)(2,1)} %gate_ref.1, bf16[192,1792]{1,0:T(8,128)(2,1)} %up_ref.1, ...), custom_call_target="tpu_custom_call" | custom-call | tf_op jit(solution)/shard_map/pallas_call | solution.py:374
  66.5 0.0 copy-start.1
  66.5 0.0 copy-start.2
  66.5 7.3 %convolution_convert_fusion = bf16[1024,1792]{1,0:T(8,128)(2,1)} fusion(bf16[768,1024]{1,0:T(8,128)(2,1)} %bitcast.6, bf16[768,3584]{1,0:T(8,128)(2,1)} %bitcast.4), kind=kOutput, calls=%fused_computation | convolution fusion | flops 2820407296 | bytes 7995392 | tf_op jit(solution)/shard_map/dot_general | solution.py:415
  73.9 0.0 copy-done.1
  73.9 0.0 copy-done.2
  73.9 0.0 copy-start
  73.9 4.5 %convolution_convert_fusion.1 = bf16[1024,1792]{1,0:T(8,128)(2,1)} fusion(bf16[768,1024]{1,0:T(8,128)(2,1)S(1)} %bitcast.7, bf16[768,3584]{1,0:T(8,128)(2,1)S(1)} %bitcast.5), kind=kOutput, calls=%fused_computation.1 | convolution fusion | flops 2820407296 | bytes 7995392 | tf_op jit(solution)/shard_map/dot_general | solution.py:412
  78.4 0.0 copy-done
  78.4 0.7 copy.10
Async XLA Ops:
  66.5 7.3 %copy-start.1 = (bf16[4,192,3584]{2,1,0:T(8,128)(2,1)S(1)}, bf16[4,192,3584]{2,1,0:T(8,128)(2,1)}, u32[]{:S(2)}) copy-start(bf16[4,192,3584]{2,1,0:T(8,128)(2,1)} %get-tuple-element.8) | copy-start | bytes 16515076
  66.5 7.3 %copy-start.2 = (bf16[4,8,24,1024]{3,2,1,0:T(8,128)(2,1)S(1)}, bf16[4,8,24,1024]{3,2,1,0:T(8,128)(2,1)}, u32[]{:S(2)}) copy-start(bf16[4,8,24,1024]{3,2,1,0:T(8,128)(2,1)} %get-tuple-element.7) | copy-start | bytes 4718596
  73.9 4.5 %copy-start = (bf16[24,4096]{1,0:T(8,128)(2,1)S(1)}, bf16[24,4096]{1,0:T(8,128)(2,1)}, u32[]{:S(2)}) copy-start(bf16[24,4096]{1,0:T(8,128)(2,1)} %get-tuple-element.12) | copy-start | bytes 589828
